TPU v7x, 256 devices: a whole 4x4x8 slice. The times are simulated.
256 devices in a mesh: src: 8 (over y, core), dst: 32 (over z, x).
Axes of the slice: x: 4, y: 4, z: 8, core: 2. Of those that a mesh axis runs over, the one named last changes fastest.
Arguments:
- features: bfloat16 [65536, 768], P(('src', 'dst')), may hold values from -6 to 6
- edge_tiles: bfloat16 [8, 32, 64, 128, 128], P('src', 'dst'), may hold values from -0.3125 to 0.3125
- tile_src: int32 [8, 32, 64], P('src', 'dst'), may hold values from 0 to 15
- tile_dst: int32 [8, 32, 64], P('src', 'dst'), may hold values from 0 to 63, as said below
- tile_count: int32 [8, 32], P('src', 'dst'), may hold values from 1 to 64, as said below
- weight: bfloat16 [768, 1024], replicated, may hold values from -0.21875 to 0.21875
- out_bias: float32 [1024], replicated, may hold values from -3 to 3
- out_grad: bfloat16 [65536, 1024], P(('src', 'dst')), may hold values from -24 to 24
Outputs:
- hidden: bfloat16 [65536, 1024], P(('src', 'dst'))
- feature_grad: bfloat16 [65536, 768], P(('src', 'dst'))
- weight_grad: float32 [768, 1024], replicated
- bias_grad: float32 [1024], replicated
Inputs may be any that keep to these rules, and one draw needn't show every extreme that they name: `tile_src`: block s of the source column of device (i, k) is block s % 2 of device (s // 2, k). `tile_dst`: block e of the destination row of device (i, k) is block e % 2 of device (i, e // 2). On one device, all tile slots whose destination blocks lie on one device name the same block. In every row of devices, slot 0 of every device names one common block. `tile_count`: some device uses all 64 slots.
All inputs are finite; a program needn't handle non-finite values.
Results may differ from a plain program's by a relative error of at most 0.024.
Values may be sent and summed in bfloat16 or wider, within the bound.
No kernel may reach another device: no remote copies, remote signals or barrier semaphores. Data moves between devices by JAX's collectives and lax.ppermute only.
A program may use at most 128 MiB of HBM per device.

v0:
```python
import jax
import jax.numpy as jnp
from jax import lax
from jax.sharding import Mesh
from jax.sharding import PartitionSpec as P

DST = ("dst_0", "dst_1")
SRC = ("src_0", "src_1")
SRC_DST = ("src_0", "src_1", "dst_0", "dst_1")


def from_everyone(x, axis):
    devices = lax.axis_size(axis)
    return lax.all_to_all(jnp.broadcast_to(x[None], (devices, *x.shape)), axis, 0, 0, tiled=True)


def laid_out(blocks, dim):
    blocks = jnp.moveaxis(blocks, 0, dim)
    lengths = blocks.shape
    return blocks.reshape(*lengths[:dim], lengths[dim] * lengths[dim + 1], *lengths[dim + 2 :])


def gather_axes(x, axes, dim):
    far, near = axes
    blocks = from_everyone(from_everyone(x, far), near)
    return laid_out(blocks.swapaxes(0, 1).reshape(-1, *x.shape), dim)


def split_up(x, dim, devices):
    lengths = x.shape
    blocks = x.reshape(*lengths[:dim], devices, lengths[dim] // devices, *lengths[dim + 1 :])
    return jnp.moveaxis(blocks, dim, 0)


def sum_at_owner(x, axis, dim):
    devices = lax.axis_size(axis)
    blocks = lax.all_to_all(split_up(x, dim, devices), axis, 0, 0, tiled=True)
    return jnp.sum(blocks.astype(jnp.float32), axis=0)


def summed_rows(x, axes, dim):
    far, near = axes
    blocks = split_up(x, dim, lax.axis_size(far))
    nearer = sum_at_owner(blocks, near, dim + 1)
    arrived = lax.all_to_all(
        nearer.astype(jnp.bfloat16), far, split_axis=0, concat_axis=0, tiled=True
    )
    return arrived.astype(jnp.float32).sum(axis=0)


def filled_up(lines, devices):
    spare = -lines.shape[0] % devices
    if not spare:
        return lines
    return jnp.concatenate([lines, jnp.zeros((spare, *lines.shape[1:]), lines.dtype)])


def total_of(x, axes):
    lines = x.reshape(-1)
    own = summed_rows(filled_up(lines, lax.axis_size(axes[0]) * lax.axis_size(axes[1])), axes, 0)
    whole = gather_axes(own.astype(jnp.bfloat16), axes, 0)
    return whole[: len(lines)].reshape(x.shape).astype(jnp.float32)


def per_device(features, edge_tiles, tile_src, tile_dst, tile_count, weight, out_bias, out_grad):
    capacity = edge_tiles.shape[2]
    edge_size = edge_tiles.shape[3]
    feat_width = features.shape[1]
    block_rows = features.shape[0]
    blocks = block_rows // edge_size
    masters = lax.axis_size(DST)
    holders = lax.axis_size(SRC)
    adjacency = edge_tiles.reshape(capacity, edge_size, edge_size)
    src_ids = tile_src.reshape(capacity)
    dst_ids = tile_dst.reshape(capacity)
    tile_total = tile_count.reshape(())
    alive_mask = jnp.arange(capacity, dtype=jnp.int32) < tile_total
    block_ids = jnp.arange(blocks, dtype=jnp.int32)
    owner_ids = dst_ids // blocks
    inner_ids = dst_ids % blocks
    column = gather_axes(features, ("src_0", "src_1"), 0).reshape(
        holders * blocks, edge_size, feat_width
    )
    picked = column[src_ids]
    partial_value = jnp.einsum(
        "tij,tjf->tif", adjacency, picked, preferred_element_type=jnp.float32
    )
    routing = (owner_ids[None, :] == jnp.arange(masters, dtype=jnp.int32)[:, None]) & alive_mask[
        None, :
    ]
    outgoing = jnp.einsum("pt,tif->pif", routing.astype(jnp.float32), partial_value)
    wanted_block = jnp.max(jnp.where(routing, inner_ids[None, :], 0), axis=1)
    wanted_rows = jnp.broadcast_to(wanted_block[:, None], (masters, edge_size))
    incoming = lax.all_to_all(
        outgoing.astype(jnp.bfloat16), DST, split_axis=0, concat_axis=0, tiled=True
    )
    asked = lax.all_to_all(wanted_rows, DST, split_axis=0, concat_axis=0, tiled=True)
    chooser = (asked[None, :, :] == block_ids[:, None, None]).astype(jnp.bfloat16)
    aggregate = jnp.einsum(
        "jpr,prf->jrf", chooser, incoming, preferred_element_type=jnp.float32
    ).astype(jnp.bfloat16)
    preact = (
        jnp.einsum("jrf,fh->jrh", aggregate, weight, preferred_element_type=jnp.float32) + out_bias
    )
    aggregate, preact, asked = (aggregate, preact, asked)
    gate_value = jax.nn.sigmoid(preact)
    hidden = (preact * gate_value).astype(jnp.bfloat16).reshape(block_rows, -1)
    grad_in = out_grad.reshape(blocks, edge_size, -1).astype(jnp.float32)
    pre_grad = grad_in * (gate_value * (1.0 + preact * (1.0 - gate_value)))
    pre_grad_b = pre_grad.astype(jnp.bfloat16)
    weight_term = jnp.einsum(
        "jrf,jrh->fh", aggregate, pre_grad_b, preferred_element_type=jnp.float32
    )
    bias_term = jnp.sum(pre_grad, axis=(0, 1))
    weight_grad, bias_grad = (
        total_of(weight_term.astype(jnp.bfloat16), (("src_0", "src_1", "dst_0"), "dst_1")),
        total_of(bias_term.astype(jnp.bfloat16), (("src_0", "src_1", "dst_0"), "dst_1")),
    )
    back = jnp.einsum("jrh,fh->jrf", pre_grad_b, weight, preferred_element_type=jnp.float32).astype(
        jnp.bfloat16
    )
    row_grads_all = lax.all_gather(back.reshape(block_rows, feat_width), DST, axis=0, tiled=True)
    wanted = row_grads_all.reshape(masters * blocks, edge_size, feat_width)[dst_ids]
    source = jnp.einsum("tji,tjf->tif", adjacency, wanted, preferred_element_type=jnp.float32)
    src_routing = (
        src_ids[None, :] == jnp.arange(holders * blocks, dtype=jnp.int32)[:, None]
    ) & alive_mask[None, :]
    src_terms = jnp.einsum("kt,tif->kif", src_routing.astype(jnp.float32), source)
    summed = summed_rows(
        src_terms.reshape(holders * block_rows, feat_width).astype(jnp.bfloat16),
        ("src_0", "src_1"),
        0,
    )
    feature_grad = summed.astype(jnp.bfloat16)
    return (hidden, feature_grad, weight_grad, bias_grad)


def solution(mesh):
    split = Mesh(mesh.devices.reshape(4, 2, 8, 4), ("src_0", "src_1", "dst_0", "dst_1"))
    in_specs = (
        P(SRC_DST, None),
        P(SRC, DST, None, None, None),
        P(SRC, DST, None),
        P(SRC, DST, None),
        P(SRC, DST),
        P(),
        P(),
        P(SRC_DST, None),
    )
    out_specs = (P(SRC_DST, None), P(SRC_DST, None), P(), P())
    return jax.shard_map(
        per_device, mesh=split, in_specs=in_specs, out_specs=out_specs, check_vma=False
    )
```

profile of v0, /device:TPU:1, one launch (start us, length us, event | category | flops | bytes accessed | tf_op | source)
XLA Modules:
  0.0 527.0 jit_solution(15362467334959138437)
XLA Ops:
  9.6 5.0 all-to-all-start
  15.4 17.7 %all-to-all-done = bf16[4,256,768]{2,1,0:T(8,128)(2,1)} async-done(((bf16[4,256,768]{2,1,0:T(8,128)(2,1)}), bf16[4,256,768]{2,1,0:T(8,128)(2,1)}, u32[]{:S(2)}, u32[]{:S(2)}) %all-to-all-start) | async-done | bytes 1572896 | tf_op jit(solution)/shard_map/all_to_all | solution.py:14
  34.8 10.1 %all_to_all.81 = bf16[2,4,256,768]{3,2,1,0:T(8,128)(2,1)} all-to-all(bf16[2,4,256,768]{3,2,1,0:T(8,128)(2,1)S(1)} %broadcast_in_dim.31), channel_id=1, replica_groups=mesh['src_0'=4,'src_1'=2,'dst_0'=8,'dst_1'=4] {'src_1'}, dimensions={0} | all-to-all | bytes 6291456 | tf_op jit(solution)/shard_map/all_to_all | solution.py:14
  45.6 11.1 %all-to-all-start.3 = ((s32[32,1,128]{2,1,0:T(1,128)}), s32[32,1,128]{2,1,0:T(1,128)S(1)}, u32[]{:S(2)}, u32[]{:S(2)}) async-start(s32[32,1,128]{2,1,0:T(1,128)} %broadcast_in_dim.34), calls=%async_computation.3 | async-start | bytes 32768 | tf_op jit(solution)/shard_map/all_to_all | solution.py:97
  60.5 9.1 %gather_fusion = bf16[64,128,768]{2,1,0:T(8,128)(2,1)} fusion(bf16[16,128,768]{2,1,0:T(8,128)(2,1)} %bitcast.97, s32[1024]{0:T(1024)S(1)} %pad_clamp_fusion.1), kind=kCustom, calls=%fused_computation | custom fusion | bytes 25166080 | tf_op jit(solution)/shard_map/gather | solution.py:84
  69.6 9.2 %convolution_bitcast_fusion.1 = bf16[64,128,768]{1,2,0:T(8,128)(2,1)} fusion(bf16[64,128,768]{2,1,0:T(8,128)(2,1)} %gather_fusion, bf16[1,1,64,128,128]{4,3,2,1,0:T(8,128)(2,1)S(1)} %copy-done), kind=kOutput, calls=%fused_computation.3 | convolution fusion | flops 1610612736 | bytes 27262976 | tf_op jit(solution)/shard_map/tij,tjf->tif/dot_general | solution.py:85
  78.8 16.7 %copy.54 = bf16[64,128,768]{2,0,1:T(8,128)(2,1)} copy(bf16[64,128,768]{1,2,0:T(8,128)(2,1)} %convolution_bitcast_fusion.1) | data formatting | bytes 25165824 | tf_op jit(solution)/shard_map/tij,tjf->tif/dot_general | solution.py:85
  95.5 6.4 %convolution_convert_fusion = bf16[32,128,768]{2,0,1:T(8,128)(2,1)S(1)} fusion(bf16[64,128,768]{2,0,1:T(8,128)(2,1)} %copy.54, s32[64]{0:T(128)S(1)} %get-tuple-element.8, pred[64]{0:T(512)(128)(4,1)S(1)} %iota_compare_fusion.2), kind=kOutput, calls=%fused_computation.6 | convolution fusion | flops 402657280 | bytes 18874688 | tf_op jit(solution)/shard_map/pt,tif->pif/dot_general | solution.py:91
  101.9 6.2 %copy.55 = bf16[32,128,768]{2,1,0:T(8,128)(2,1)} copy(bf16[32,128,768]{2,0,1:T(8,128)(2,1)S(1)} %convolution_convert_fusion) | data formatting | bytes 12582912 | tf_op jit(solution)/shard_map/convert_element_type | solution.py:95
  108.1 9.3 %all-to-all-start.2 = ((bf16[32,128,768]{2,1,0:T(8,128)(2,1)}), bf16[32,128,768]{2,1,0:T(8,128)(2,1)}, u32[]{:S(2)}, u32[]{:S(2)}) async-start(bf16[32,128,768]{2,1,0:T(8,128)(2,1)} %copy.55), calls=%async_computation.2 | async-start | bytes 12582912 | tf_op jit(solution)/shard_map/all_to_all | solution.py:94
  117.8 138.2 %all-to-all-done.2 = bf16[32,128,768]{2,1,0:T(8,128)(2,1)} async-done(((bf16[32,128,768]{2,1,0:T(8,128)(2,1)}), bf16[32,128,768]{2,1,0:T(8,128)(2,1)}, u32[]{:S(2)}, u32[]{:S(2)}) %all-to-all-start.2) | async-done | bytes 6291488 | tf_op jit(solution)/shard_map/all_to_all | solution.py:94
  256.0 7.5 %fusion.17 = bf16[2,128,768]{2,0,1:T(2,128)(2,1)S(1)} fusion(bf16[32,128,768]{2,1,0:T(8,128)(2,1)} %all-to-all-done.2, s32[32,128]{0,1:T(8,128)S(1)} %copy.56), kind=kOutput, calls=%fused_computation.20 | convolution fusion | flops 12787712 | bytes 6701056 | tf_op jit(solution)/shard_map/jpr,prf->jrf/dot_general | solution.py:99
  269.8 9.3 %all-to-all-start.10 = ((bf16[4,2,128]{2,1,0:T(2,128)(2,1)}), bf16[4,2,128]{2,1,0:T(2,128)(2,1)S(1)}, u32[]{:S(2)}, u32[]{:S(2)}) async-start(bf16[4,2,128]{2,1,0:T(2,128)(2,1)} %reshape.219), calls=%async_computation.10 | async-start | bytes 4096 | tf_op jit(solution)/shard_map/all_to_all | solution.py:37
  293.4 21.4 %all-to-all-done.6 = bf16[4,64,3072]{2,1,0:T(8,128)(2,1)} async-done(((bf16[4,64,3072]{2,1,0:T(8,128)(2,1)}), bf16[4,64,3072]{2,1,0:T(8,128)(2,1)}, u32[]{:S(2)}, u32[]{:S(2)}) %all-to-all-start.6) | async-done | bytes 1572896 | tf_op jit(solution)/shard_map/all_to_all | solution.py:37
  314.8 8.8 %all-to-all-start.11 = ((bf16[64,1,4]{2,1,0:T(2,128)(2,1)}), bf16[64,1,4]{2,1,0:T(2,128)(2,1)S(1)}, u32[]{:S(2)}, u32[]{:S(2)}) async-start(bf16[64,1,4]{2,1,0:T(2,128)(2,1)} %copy.68), calls=%async_computation.11 | async-start | bytes 65536 | tf_op jit(solution)/shard_map/all_to_all | solution.py:45
  327.7 5.2 all-to-all-done.11
  332.9 5.3 %all-to-all-start.7 = ((bf16[64,2,1536]{2,1,0:T(2,128)(2,1)}), bf16[64,2,1536]{2,1,0:T(2,128)(2,1)S(1)}, u32[]{:S(2)}, u32[]{:S(2)}) async-start(bf16[64,2,1536]{2,1,0:T(2,128)(2,1)} %reshape.215), calls=%async_computation.7 | async-start | bytes 786432 | tf_op jit(solution)/shard_map/all_to_all | solution.py:45
  338.3 18.9 %all-to-all-done.7 = bf16[64,2,1536]{2,1,0:T(2,128)(2,1)S(1)} async-done(((bf16[64,2,1536]{2,1,0:T(2,128)(2,1)}), bf16[64,2,1536]{2,1,0:T(2,128)(2,1)S(1)}, u32[]{:S(2)}, u32[]{:S(2)}) %all-to-all-start.7) | async-done | bytes 393248 | tf_op jit(solution)/shard_map/all_to_all | solution.py:45
  357.9 6.5 %all-to-all-start.12 = ((bf16[64,1,4]{2,1,0:T(2,128)(2,1)}), bf16[64,1,4]{2,1,0:T(2,128)(2,1)S(1)}, u32[]{:S(2)}, u32[]{:S(2)}) async-start(bf16[64,1,4]{2,1,0:T(2,128)(2,1)} %broadcast_in_dim.38), calls=%async_computation.12 | async-start | bytes 65536 | tf_op jit(solution)/shard_map/all_to_all | solution.py:14
  373.9 6.3 %all-to-all-start.8 = ((bf16[64,2,1536]{2,1,0:T(2,128)(2,1)}), bf16[64,2,1536]{2,1,0:T(2,128)(2,1)S(1)}, u32[]{:S(2)}, u32[]{:S(2)}) async-start(bf16[64,2,1536]{2,1,0:T(2,128)(2,1)} %reshape.217), calls=%async_computation.8 | async-start | bytes 786432 | tf_op jit(solution)/shard_map/all_to_all | solution.py:14
  381.0 18.1 %all-to-all-done.8 = bf16[64,2,1536]{2,1,0:T(2,128)(2,1)S(1)} async-done(((bf16[64,2,1536]{2,1,0:T(2,128)(2,1)}), bf16[64,2,1536]{2,1,0:T(2,128)(2,1)S(1)}, u32[]{:S(2)}, u32[]{:S(2)}) %all-to-all-start.8) | async-done | bytes 393248 | tf_op jit(solution)/shard_map/all_to_all | solution.py:14
  403.0 6.4 %all-gather.2.cloned.1.call-done = bf16[8192,768]{1,0:T(8,128)(2,1)} async-done(((bf16[256,768]{1,0:T(8,128)(2,1)}), bf16[8192,768]{1,0:T(8,128)(2,1)}) %all-gather.2.cloned.1.call-update) | async-done | bytes 12582928 | tf_op jit(solution)/shard_map/all_gather | solution.py:122
  409.4 11.7 %gather_fusion.1 = bf16[64,128,768]{2,1,0:T(8,128)(2,1)} fusion(bf16[64,128,768]{2,1,0:T(8,128)(2,1)} %bitcast.99, s32[1024]{0:T(1024)S(1)} %pad_clamp_fusion), kind=kCustom, calls=%fused_computation.1 | custom fusion | bytes 25166080 | tf_op jit(solution)/shard_map/gather | solution.py:123
  421.1 9.2 %convolution_bitcast_fusion = bf16[64,128,768]{1,2,0:T(8,128)(2,1)} fusion(bf16[64,128,768]{2,1,0:T(8,128)(2,1)} %gather_fusion.1, bf16[1,1,64,128,128]{4,3,2,1,0:T(8,128)(2,1)S(1)} %copy-done), kind=kOutput, calls=%fused_computation.2 | convolution fusion | flops 1610612736 | bytes 27262976 | tf_op jit(solution)/shard_map/tji,tjf->tif/dot_general | solution.py:124
  430.3 16.7 %copy.60 = bf16[64,128,768]{2,0,1:T(8,128)(2,1)} copy(bf16[64,128,768]{1,2,0:T(8,128)(2,1)} %convolution_bitcast_fusion) | data formatting | bytes 25165824 | tf_op jit(solution)/shard_map/tji,tjf->tif/dot_general | solution.py:124
  447.0 6.3 %convolution_convert_fusion.1 = bf16[16,128,768]{2,0,1:T(8,128)(2,1)S(1)} fusion(bf16[64,128,768]{2,0,1:T(8,128)(2,1)} %copy.60, s32[64]{0:T(128)S(1)} %bitcast.109, pred[64]{0:T(512)(128)(4,1)S(1)} %iota_compare_fusion.2), kind=kOutput, calls=%fused_computation.9 | convolution fusion | flops 201328640 | bytes 15728960 | tf_op jit(solution)/shard_map/kt,tif->kif/dot_general | solution.py:128
  456.2 10.8 %all_to_all.82 = bf16[2,4,256,768]{3,2,1,0:T(8,128)(2,1)} all-to-all(bf16[2,4,256,768]{3,2,1,0:T(8,128)(2,1)} %copy.62), channel_id=1, replica_groups=mesh['src_0'=4,'src_1'=2,'dst_0'=8,'dst_1'=4] {'src_1'}, dimensions={0} | all-to-all | bytes 6291456 | tf_op jit(solution)/shard_map/all_to_all | solution.py:37
  468.4 4.4 all-to-all-start.9
  476.7 16.5 %all-to-all-done.9 = bf16[4,64,3072]{2,1,0:T(8,128)(2,1)} async-done(((bf16[4,64,3072]{2,1,0:T(8,128)(2,1)}), bf16[4,64,3072]{2,1,0:T(8,128)(2,1)}, u32[]{:S(2)}, u32[]{:S(2)}) %all-to-all-start.9) | async-done | bytes 1572896 | tf_op jit(solution)/shard_map/all_to_all | solution.py:14
  493.2 4.6 all-to-all-start.5
  504.2 5.1 reshape.193
  509.3 8.1 %all-to-all-done.5 = bf16[4,256,768]{2,1,0:T(8,128)(2,1)} async-done(((bf16[4,256,768]{2,1,0:T(8,128)(2,1)}), bf16[4,256,768]{2,1,0:T(8,128)(2,1)}, u32[]{:S(2)}, u32[]{:S(2)}) %all-to-all-start.5) | async-done | bytes 1572896 | tf_op jit(solution)/shard_map/all_to_all | solution.py:45
  (69 shorter events, 65.5 us)
Async XLA Ops:
  7.2 62.4 %copy-start = (bf16[1,1,64,128,128]{4,3,2,1,0:T(8,128)(2,1)S(1)}, bf16[1,1,64,128,128]{4,3,2,1,0:T(8,128)(2,1)}, u32[]{:S(2)}) copy-start(bf16[1,1,64,128,128]{4,3,2,1,0:T(8,128)(2,1)} %param.9) | copy-start | bytes 6291460
  7.2 8.1 %copy-start.1 = (s32[1,1,64]{2,1,0:T(1,128)S(1)}, s32[1,1,64]{2,1,0:T(1,128)}, u32[]{:S(2)}) copy-start(s32[1,1,64]{2,1,0:T(1,128)} %param.10) | copy-start | bytes 772
  7.2 8.1 %copy-start.4 = (s32[1,1,64]{2,1,0:T(1,128)S(1)}, s32[1,1,64]{2,1,0:T(1,128)}, u32[]{:S(2)}) copy-start(s32[1,1,64]{2,1,0:T(1,128)} %param.11) | copy-start | bytes 772
  9.6 23.6 %all-to-all-start = ((bf16[4,256,768]{2,1,0:T(8,128)(2,1)}), bf16[4,256,768]{2,1,0:T(8,128)(2,1)}, u32[]{:S(2)}, u32[]{:S(2)}) async-start(bf16[4,256,768]{2,1,0:T(8,128)(2,1)} %broadcast_in_dim.30), calls=%async_computation | async-start | bytes 3145728 | tf_op jit(solution)/shard_map/all_to_all | solution.py:14
  45.6 62.5 %all-to-all-start.3 = ((s32[32,1,128]{2,1,0:T(1,128)}), s32[32,1,128]{2,1,0:T(1,128)S(1)}, u32[]{:S(2)}, u32[]{:S(2)}) async-start(s32[32,1,128]{2,1,0:T(1,128)} %broadcast_in_dim.34), calls=%async_computation.3 | async-start | bytes 32768 | tf_op jit(solution)/shard_map/all_to_all | solution.py:97
  108.1 147.9 %all-to-all-start.2 = ((bf16[32,128,768]{2,1,0:T(8,128)(2,1)}), bf16[32,128,768]{2,1,0:T(8,128)(2,1)}, u32[]{:S(2)}, u32[]{:S(2)}) async-start(bf16[32,128,768]{2,1,0:T(8,128)(2,1)} %copy.55), calls=%async_computation.2 | async-start | bytes 12582912 | tf_op jit(solution)/shard_map/all_to_all | solution.py:94
  117.5 292.0 %all-gather.2.cloned.1.call-start = ((), (), s32[]{:S(2)}) async-start(), calls=%async_computation.14 | async-start | bytes 12976128 | tf_op jit(solution)/shard_map/all_gather | solution.py:122
  117.8 146.2 %copy-start.3 = (f32[1024]{0:T(1024)S(1)}, f32[1024]{0:T(1024)}, u32[]{:S(2)}) copy-start(f32[1024]{0:T(1024)} %param.14) | copy-start | bytes 12292
  264.0 3.4 copy-start.2
  269.8 18.4 %all-to-all-start.10 = ((bf16[4,2,128]{2,1,0:T(2,128)(2,1)}), bf16[4,2,128]{2,1,0:T(2,128)(2,1)S(1)}, u32[]{:S(2)}, u32[]{:S(2)}) async-start(bf16[4,2,128]{2,1,0:T(2,128)(2,1)} %reshape.219), calls=%async_computation.10 | async-start | bytes 4096 | tf_op jit(solution)/shard_map/all_to_all | solution.py:37
  288.3 26.6 %all-to-all-start.6 = ((bf16[4,64,3072]{2,1,0:T(8,128)(2,1)}), bf16[4,64,3072]{2,1,0:T(8,128)(2,1)}, u32[]{:S(2)}, u32[]{:S(2)}) async-start(bf16[4,64,3072]{2,1,0:T(8,128)(2,1)} %bitcast.100), calls=%async_computation.6 | async-start | bytes 3145728 | tf_op jit(solution)/shard_map/all_to_all | solution.py:37
  314.8 18.1 %all-to-all-start.11 = ((bf16[64,1,4]{2,1,0:T(2,128)(2,1)}), bf16[64,1,4]{2,1,0:T(2,128)(2,1)S(1)}, u32[]{:S(2)}, u32[]{:S(2)}) async-start(bf16[64,1,4]{2,1,0:T(2,128)(2,1)} %copy.68), calls=%async_computation.11 | async-start | bytes 65536 | tf_op jit(solution)/shard_map/all_to_all | solution.py:45
  332.9 24.3 %all-to-all-start.7 = ((bf16[64,2,1536]{2,1,0:T(2,128)(2,1)}), bf16[64,2,1536]{2,1,0:T(2,128)(2,1)S(1)}, u32[]{:S(2)}, u32[]{:S(2)}) async-start(bf16[64,2,1536]{2,1,0:T(2,128)(2,1)} %reshape.215), calls=%async_computation.7 | async-start | bytes 786432 | tf_op jit(solution)/shard_map/all_to_all | solution.py:45
  357.9 16.0 %all-to-all-start.12 = ((bf16[64,1,4]{2,1,0:T(2,128)(2,1)}), bf16[64,1,4]{2,1,0:T(2,128)(2,1)S(1)}, u32[]{:S(2)}, u32[]{:S(2)}) async-start(bf16[64,1,4]{2,1,0:T(2,128)(2,1)} %broadcast_in_dim.38), calls=%async_computation.12 | async-start | bytes 65536 | tf_op jit(solution)/shard_map/all_to_all | solution.py:14
  373.9 25.2 %all-to-all-start.8 = ((bf16[64,2,1536]{2,1,0:T(2,128)(2,1)}), bf16[64,2,1536]{2,1,0:T(2,128)(2,1)S(1)}, u32[]{:S(2)}, u32[]{:S(2)}) async-start(bf16[64,2,1536]{2,1,0:T(2,128)(2,1)} %reshape.217), calls=%async_computation.8 | async-start | bytes 786432 | tf_op jit(solution)/shard_map/all_to_all | solution.py:14
  399.1 57.1 %all-to-all-start.13 = ((bf16[4,2,128]{2,1,0:T(2,128)(2,1)}), bf16[4,2,128]{2,1,0:T(2,128)(2,1)S(1)}, u32[]{:S(2)}, u32[]{:S(2)}) async-start(bf16[4,2,128]{2,1,0:T(2,128)(2,1)} %reshape.221), calls=%async_computation.13 | async-start | bytes 4096 | tf_op jit(solution)/shard_map/all_to_all | solution.py:14
  468.4 24.9 %all-to-all-start.9 = ((bf16[4,64,3072]{2,1,0:T(8,128)(2,1)}), bf16[4,64,3072]{2,1,0:T(8,128)(2,1)}, u32[]{:S(2)}, u32[]{:S(2)}) async-start(bf16[4,64,3072]{2,1,0:T(8,128)(2,1)} %broadcast_in_dim.37), calls=%async_computation.9 | async-start | bytes 3145728 | tf_op jit(solution)/shard_map/all_to_all | solution.py:14
  493.2 24.2 %all-to-all-start.5 = ((bf16[4,256,768]{2,1,0:T(8,128)(2,1)}), bf16[4,256,768]{2,1,0:T(8,128)(2,1)}, u32[]{:S(2)}, u32[]{:S(2)}) async-start(bf16[4,256,768]{2,1,0:T(8,128)(2,1)} %reduce_sum.81), calls=%async_computation.5 | async-start | bytes 3145728 | tf_op jit(solution)/shard_map/all_to_all | solution.py:45
Sparse Core Ops, SparseCore 0:
  269.0 140.4 all-gather.1
where the time goes:
time: 537 us; the launch traced here: 527 us
  waiting for transfers between devices  255 us (47%)
  local copies, waits for them, and re-layouts  97.7 us (18%)
  starting transfers between devices  78.6 us (15%)
  matrix products  45.2 us (8%)
  blocking collectives  20.9 us (4%)
  between operations  15.2 us (3%)
  other arithmetic  14.8 us (3%)
    all_to_all x1, waiting for transfers between devices, per_device(): lax.all_to_all(outgoing.astype(jnp.bfloat16), DST, split_axis=0, concat_a...  138 us
    all_to_all x5, waiting for transfers between devices, from_everyone(): lax.all_to_all(jnp.broadcast_to(x[None], (devices, *x.shape)), axis, 0, 0...  56.4 us
    all_to_all x3, waiting for transfers between devices, summed_rows(): lax.all_to_all(nearer.astype(jnp.bfloat16), far, split_axis=0, concat_axi...  32.2 us
    all_to_all x5, starting transfers between devices, from_everyone(): lax.all_to_all(jnp.broadcast_to(x[None], (devices, *x.shape)), axis, 0, 0...  25.6 us
    all_to_all x2, waiting for transfers between devices, sum_at_owner(): blocks = lax.all_to_all(split_up(x, dim, devices), axis, 0, 0, tiled=True)  21.4 us
    all_to_all x3, starting transfers between devices, summed_rows(): lax.all_to_all(nearer.astype(jnp.bfloat16), far, split_axis=0, concat_axi...  18.7 us
    dot_general x1, local copies, waits for them, and re-layouts, per_device(): jnp.einsum('tij,tjf->tif', adjacency, picked, preferred_element_type=jnp....  16.7 us
    dot_general x1, local copies, waits for them, and re-layouts, per_device(): jnp.einsum('tji,tjf->tif', adjacency, wanted, preferred_element_type=jnp....  16.7 us
  transfers between devices with their start and end apart: 13, of which 10 were waited for; matrix products, arithmetic and copies ran while one was open for 26% of the time, Pallas kernels for 0%

commit v1 on v0

v1 whole, which is shorter than its diff:
```python
import functools

import jax
import jax.numpy as jnp
from jax import lax
from jax.experimental import pallas as pl
from jax.experimental.pallas import tpu as pltpu
from jax.sharding import Mesh
from jax.sharding import PartitionSpec as P

SRC = ("y", "c")
DST = ("z", "x")
ALL = ("y", "c", "z", "x")
CHUNKS = 2
SMEM = pl.BlockSpec(memory_space=pltpu.SMEM)
VMEM = pl.BlockSpec(memory_space=pltpu.VMEM)


def link_tiles(key_of, count, head, nxt, groups):
    def clear(g, _):
        head[g] = -1
        return 0

    lax.fori_loop(0, groups, clear, 0)

    def push(t, _):
        g = key_of(t)
        nxt[t] = head[g]
        head[g] = t
        return 0

    lax.fori_loop(0, count, push, 0)


def walk(head, nxt, g, pair, acc):
    def one(t):
        t2 = nxt[t]
        has = t2 >= 0
        t2 = jnp.maximum(t2, 0)
        return pair(t, t2, has), jnp.where(has, nxt[t2], -1)

    value, t = one(head[g])
    acc[...] = value

    def more(t):
        value, t = one(t)
        acc[...] += value
        return t

    lax.while_loop(lambda t: t >= 0, more, t)


def forward_kernel(src, dst, count, adj, col, *rest, blocks, nx, chunks):
    outs, (head, nxt, acc) = rest[:chunks], rest[chunks:]
    nz = outs[0].shape[1]
    rows = outs[0].shape[2]
    link_tiles(lambda t: dst[t] // blocks, count[0], head, nxt, nx * nz)

    def pair(t, t2, has):
        second = adj[t2]
        second = jnp.where(has, second, jnp.zeros_like(second))
        left = jnp.concatenate([adj[t], second], axis=1)
        right = jnp.concatenate([col[src[t]], col[src[t2]]], axis=0)
        return jnp.dot(left, right, preferred_element_type=jnp.float32)

    def master(m, _):
        xi = lax.rem(m, nx)
        zi = m // nx

        @pl.when(head[m] < 0)
        def _():
            for out in outs:
                out[xi, zi] = jnp.zeros(out.shape[2:], out.dtype)

        @pl.when(head[m] >= 0)
        def _():
            walk(head, nxt, m, pair, acc)
            for r, out in enumerate(outs):
                out[xi, zi] = acc[r * rows : (r + 1) * rows].astype(out.dtype)

        return 0

    lax.fori_loop(0, nx * nz, master, 0)


def forward_products(src_ids, dst_ids, count, adj, col, blocks, nx, nz, chunks):
    tiles, size, _ = adj.shape
    width = col.shape[2]
    rows = size // chunks
    return pl.pallas_call(
        functools.partial(forward_kernel, blocks=blocks, nx=nx, chunks=chunks),
        out_shape=[jax.ShapeDtypeStruct((nx, nz, rows, width), jnp.bfloat16)] * chunks,
        in_specs=[SMEM, SMEM, SMEM, VMEM, VMEM],
        out_specs=[VMEM] * chunks,
        scratch_shapes=[
            pltpu.SMEM((nx * nz,), jnp.int32),
            pltpu.SMEM((tiles,), jnp.int32),
            pltpu.VMEM((size, width), jnp.float32),
        ],
        compiler_params=pltpu.CompilerParams(vmem_limit_bytes=48 * 1024 * 1024),
        cost_estimate=pl.CostEstimate(
            flops=2 * tiles * size * size * width, transcendentals=0, bytes_accessed=12_000_000
        ),
        name="forward_products",
    )(src_ids, dst_ids, count, adj, col)


def backward_kernel(src, dst, count, adj, *rest, blocks, nx, chunks):
    wanted, out, (head, nxt, acc) = rest[:chunks], rest[chunks], rest[chunks + 1 :]
    groups = out.shape[0]
    link_tiles(lambda t: src[t], count[0], head, nxt, groups)

    def rows_of(t):
        m = dst[t] // blocks
        xi = lax.rem(m, nx)
        zi = m // nx
        return [w[xi, zi] for w in wanted]

    def pair(t, t2, has):
        second = adj[t2]
        second = jnp.where(has, second, jnp.zeros_like(second))
        left = jnp.concatenate([adj[t], second], axis=0)
        right = jnp.concatenate(rows_of(t) + rows_of(t2), axis=0)
        return lax.dot_general(
            left, right, (((0,), (0,)), ((), ())), preferred_element_type=jnp.float32
        )

    def block(s, _):
        @pl.when(head[s] < 0)
        def _():
            out[s] = jnp.zeros(out.shape[1:], out.dtype)

        @pl.when(head[s] >= 0)
        def _():
            walk(head, nxt, s, pair, acc)
            out[s] = acc[...].astype(out.dtype)

        return 0

    lax.fori_loop(0, groups, block, 0)


def backward_products(src_ids, dst_ids, count, adj, wanted, blocks, groups):
    tiles, size, _ = adj.shape
    nx, _, _, width = wanted[0].shape
    chunks = len(wanted)
    return pl.pallas_call(
        functools.partial(backward_kernel, blocks=blocks, nx=nx, chunks=chunks),
        out_shape=jax.ShapeDtypeStruct((groups, size, width), jnp.bfloat16),
        in_specs=[SMEM, SMEM, SMEM, VMEM] + [VMEM] * chunks,
        out_specs=VMEM,
        scratch_shapes=[
            pltpu.SMEM((groups,), jnp.int32),
            pltpu.SMEM((tiles,), jnp.int32),
            pltpu.VMEM((size, width), jnp.float32),
        ],
        compiler_params=pltpu.CompilerParams(vmem_limit_bytes=48 * 1024 * 1024),
        cost_estimate=pl.CostEstimate(
            flops=2 * tiles * size * size * width, transcendentals=0, bytes_accessed=12_000_000
        ),
        name="backward_products",
    )(src_ids, dst_ids, count, adj, *wanted)


def combine_kernel(asked, arrived, out):
    z = pl.program_id(0)
    nx = arrived.shape[0]
    values = [arrived[x, 0].astype(jnp.float32) for x in range(nx)]
    for j in range(out.shape[1]):
        total = jnp.zeros(values[0].shape, jnp.float32)
        for x in range(nx):
            total += jnp.where(asked[x, z] == j, values[x], 0.0)
        out[0, j] = total.astype(out.dtype)


def combine(asked, arrived, blocks):
    nx, nz, rows, width = arrived.shape
    return pl.pallas_call(
        combine_kernel,
        grid=(nz,),
        out_shape=jax.ShapeDtypeStruct((nz, blocks, rows, width), jnp.bfloat16),
        in_specs=[SMEM, pl.BlockSpec((nx, 1, rows, width), lambda z: (0, z, 0, 0))],
        out_specs=pl.BlockSpec((1, blocks, rows, width), lambda z: (z, 0, 0, 0)),
        cost_estimate=pl.CostEstimate(
            flops=8 * nx * nz * rows * width, transcendentals=0, bytes_accessed=6_000_000
        ),
        name="combine",
    )(asked, arrived)


def pick_kernel(asked, held, out):
    z = pl.program_id(0)
    for x in range(out.shape[0]):
        out[x, 0] = held[0, asked[x, z]]


def pick(asked, held, nx):
    nz, blocks, rows, width = held.shape
    return pl.pallas_call(
        pick_kernel,
        grid=(nz,),
        out_shape=jax.ShapeDtypeStruct((nx, nz, rows, width), jnp.bfloat16),
        in_specs=[SMEM, pl.BlockSpec((1, blocks, rows, width), lambda z: (z, 0, 0, 0))],
        out_specs=pl.BlockSpec((nx, 1, rows, width), lambda z: (0, z, 0, 0)),
        cost_estimate=pl.CostEstimate(
            flops=nx * nz * rows * width, transcendentals=0, bytes_accessed=6_000_000
        ),
        name="pick",
    )(asked, held)


def reduced_grads(weight_term, bias_term):
    feat, hidden = weight_term.shape
    src = lax.axis_size(SRC)
    dst = lax.axis_size(DST)
    part = feat // src // dst
    own = lax.psum_scatter(
        weight_term.astype(jnp.bfloat16), SRC, scatter_dimension=0, tiled=True
    )
    bias = bias_term.astype(jnp.bfloat16).reshape(dst, 1, hidden // dst)
    bias = jnp.pad(bias, ((0, 0), (0, 0), (0, hidden - hidden // dst)))
    lines = jnp.concatenate([own.reshape(dst, part, hidden), bias], axis=1)
    arrived = lax.all_to_all(lines, DST, 0, 0, tiled=True)
    summed = jnp.sum(arrived.astype(jnp.float32), axis=0).astype(jnp.bfloat16)
    shared = lax.all_to_all(
        jnp.broadcast_to(summed[None], (dst, *summed.shape)), DST, 0, 0, tiled=True
    )
    mine = shared[:, :part].reshape(dst * part, hidden)
    bias = shared[:, part, : hidden // dst].reshape(1, hidden)
    mine = jnp.concatenate([mine, jnp.pad(bias, ((0, 15), (0, 0)))], axis=0)
    whole = lax.all_gather(mine, SRC, axis=0).astype(jnp.float32)
    weight_grad = whole[:, : dst * part].reshape(feat, hidden)
    return weight_grad, jnp.sum(whole[:, dst * part], axis=0)


def per_device(features, edge_tiles, tile_src, tile_dst, tile_count, weight, out_bias, out_grad):
    capacity, size = edge_tiles.shape[2:4]
    block_rows, feat_width = features.shape
    blocks = block_rows // size
    nx, nz = lax.axis_size("x"), lax.axis_size("z")
    masters = nx * nz
    holders = lax.axis_size(SRC)
    rows = size // CHUNKS
    adj = edge_tiles.reshape(capacity, size, size)
    src_ids = tile_src.reshape(capacity)
    dst_ids = tile_dst.reshape(capacity)
    count = tile_count.reshape(1)

    alive = jnp.arange(capacity, dtype=jnp.int32) < count[0]
    routing = (dst_ids // blocks)[None, :] == jnp.arange(masters, dtype=jnp.int32)[:, None]
    inner = jnp.where(routing & alive[None, :], (dst_ids % blocks)[None, :], 0)
    wanted = jnp.max(inner, axis=1).reshape(nz, nx).T
    asked = lax.all_to_all(
        jnp.broadcast_to(wanted[:, :, None], (nx, nz, 128)), "x", 0, 0, tiled=True
    )[:, :, 0]

    column = lax.all_gather(features, SRC, axis=0, tiled=True)
    column = column.reshape(holders * blocks, size, feat_width)
    outgoing = forward_products(
        src_ids, dst_ids, count, adj, column, blocks, nx, nz, CHUNKS
    )

    grads = out_grad.reshape(blocks, size, -1)
    hidden, aggregates, pre_grads, bias_term, received = [], [], [], 0.0, []
    for r in range(CHUNKS):
        arrived = lax.all_to_all(outgoing[r], "x", 0, 0, tiled=True)
        merged = combine(asked, arrived, blocks)
        aggregate = lax.psum_scatter(
            merged.reshape(nz * blocks * rows, feat_width), "z", scatter_dimension=0, tiled=True
        )
        preact = jnp.dot(aggregate, weight, preferred_element_type=jnp.float32) + out_bias
        gate = jax.nn.sigmoid(preact)
        hidden.append((preact * gate).astype(jnp.bfloat16).reshape(blocks, rows, -1))
        grad_in = grads[:, r * rows : (r + 1) * rows].reshape(blocks * rows, -1)
        pre_grad = grad_in.astype(jnp.float32) * (gate * (1.0 + preact * (1.0 - gate)))
        pre_grad_b = pre_grad.astype(jnp.bfloat16)
        bias_term += jnp.sum(pre_grad, axis=0)
        aggregates.append(aggregate)
        pre_grads.append(pre_grad_b)
        back = lax.dot_general(
            pre_grad_b, weight, (((1,), (1,)), ((), ())), preferred_element_type=jnp.float32
        ).astype(jnp.bfloat16)
        held = lax.all_gather(back, "z", axis=0, tiled=True)
        chosen = pick(asked, held.reshape(nz, blocks, rows, feat_width), nx)
        received.append(lax.all_to_all(chosen, "x", 0, 0, tiled=True))

    weight_term = lax.dot_general(
        jnp.concatenate(aggregates, axis=0),
        jnp.concatenate(pre_grads, axis=0),
        (((0,), (0,)), ((), ())),
        preferred_element_type=jnp.float32,
    )
    weight_grad, bias_grad = reduced_grads(weight_term, bias_term)

    source = backward_products(
        src_ids, dst_ids, count, adj, received, blocks, holders * blocks
    )
    feature_grad = lax.psum_scatter(
        source.reshape(holders * block_rows, feat_width), SRC, scatter_dimension=0, tiled=True
    )
    hidden = jnp.concatenate(hidden, axis=1).reshape(block_rows, -1)
    return (hidden, feature_grad, weight_grad, bias_grad)


def solution(mesh):
    split = Mesh(mesh.devices.reshape(4, 2, 8, 4), ALL)
    in_specs = (
        P(ALL, None),
        P(SRC, DST, None, None, None),
        P(SRC, DST, None),
        P(SRC, DST, None),
        P(SRC, DST),
        P(),
        P(),
        P(ALL, None),
    )
    out_specs = (P(ALL, None), P(ALL, None), P(), P())
    return jax.shard_map(
        per_device, mesh=split, in_specs=in_specs, out_specs=out_specs, check_vma=False
    )
```

time: 537 us -> 422 us (0.79)
  local copies, waits for them, and re-layouts: 97.7 us -> 14.6 us
  blocking collectives: 20.9 us -> 99.8 us
  starting transfers between devices: 78.6 us -> 20.1 us
  matrix products: 45.2 us -> 7.39 us
  Pallas kernels: 0 us -> 36.7 us
  waiting for transfers between devices: 255 us -> 220 us
  other arithmetic: 14.8 us -> 3.65 us
    all_to_all x12 -> x4, waiting for transfers between devices: 248 us -> 37.1 us  [the longest x1 37.1 us: per_device(): arrived = lax.all_to_all(outgoing[r], 'x', 0, 0, tiled=True)]
    reduce_scatter x0 -> x4, waiting for transfers between devices: none -> 105 us  [the longest x1 38.3 us: per_device(): lax.psum_scatter(source.reshape(holders * block_rows, feat_width), SRC, s...]
    all_to_all x2 -> x3, blocking collectives: 20.9 us -> 99.8 us  [the longest x1 41.8 us: per_device(): arrived = lax.all_to_all(outgoing[r], 'x', 0, 0, tiled=True)]
    all_gather x1 -> x4, waiting for transfers between devices: 6.44 us -> 77 us  [the longest x2 47.7 us: per_device(): held = lax.all_gather(back, 'z', axis=0, tiled=True)]
    all_to_all x12 -> x4, starting transfers between devices: 78.3 us -> 19.8 us  [the longest x1 6.41 us: per_device(): arrived = lax.all_to_all(outgoing[r], 'x', 0, 0, tiled=True)]
    dot_general x8 -> x5, matrix products: 45.2 us -> 7.39 us  [the longest x2 2.96 us: per_device(): jnp.dot(aggregate, weight, preferred_element_type=jnp.float32) + out_bias]
    pallas_call x0 -> x6, Pallas kernels: none -> 36.7 us  [the longest x2 12.5 us: combine(): pl.pallas_call(combine_kernel, grid=(nz,), out_shape=jax.ShapeDtypeStruct...]
    dot_general x2 -> x0, local copies, waits for them, and re-layouts: 33.4 us -> none  [the longest x1 16.7 us: per_device(): jnp.einsum('tij,tjf->tif', adjacency, picked, preferred_element_type=jnp....]
  transfers between devices with their start and end apart: 13 -> 12, of which waited for: 10 -> 7; matrix products, arithmetic and copies ran while one was open for 26% -> 4% of each run, Pallas kernels for 0% -> 7%
where the time goes in v1:
time: 422 us; the launch traced here: 417 us
  waiting for transfers between devices  220 us (52%)
  blocking collectives  99.8 us (24%)
  Pallas kernels  36.7 us (9%)
  starting transfers between devices  20.1 us (5%)
  between operations  14.9 us (4%)
  local copies, waits for them, and re-layouts  14.6 us (3%)
  matrix products  7.39 us (2%)
    all_gather x2, waiting for transfers between devices, per_device(): held = lax.all_gather(back, 'z', axis=0, tiled=True)  47.7 us
    all_to_all x1, blocking collectives, per_device(): arrived = lax.all_to_all(outgoing[r], 'x', 0, 0, tiled=True)  41.8 us
    all_to_all x1, blocking collectives, per_device(): received.append(lax.all_to_all(chosen, 'x', 0, 0, tiled=True))  38.6 us
    reduce_scatter x1, waiting for transfers between devices, per_device(): lax.psum_scatter(source.reshape(holders * block_rows, feat_width), SRC, s...  38.3 us
    all_to_all x1, waiting for transfers between devices, per_device(): arrived = lax.all_to_all(outgoing[r], 'x', 0, 0, tiled=True)  37.1 us
    reduce_scatter x2, waiting for transfers between devices, per_device(): lax.psum_scatter(merged.reshape(nz * blocks * rows, feat_width), 'z', sca...  33.9 us
    reduce_scatter x1, waiting for transfers between devices, reduced_grads(): lax.psum_scatter(weight_term.astype(jnp.bfloat16), SRC, scatter_dimension...  32.9 us
    all_gather x1, waiting for transfers between devices, per_device(): column = lax.all_gather(features, SRC, axis=0, tiled=True)  29.3 us
  transfers between devices with their start and end apart: 12, of which 7 were waited for; matrix products, arithmetic and copies ran while one was open for 4% of the time, Pallas kernels for 7%

profile of v1, /device:TPU:1, one launch (start us, length us, event | category | flops | bytes accessed | tf_op | source)
XLA Modules:
  0.0 417.1 jit_solution(8159834869035910046)
XLA Ops:
  10.2 4.8 %all-to-all-start = ((s32[4,8,128]{2,1,0:T(8,128)}), s32[4,8,128]{2,1,0:T(8,128)S(1)}, u32[]{:S(2)}, u32[]{:S(2)}) async-start(s32[4,8,128]{2,1,0:T(8,128)} %broadcast_in_dim.18), calls=%async_computation | async-start | bytes 32768 | tf_op jit(solution)/shard_map/all_to_all | solution.py:253
  15.0 29.3 %all-gather.6.cloned.1.call-done = bf16[2048,768]{1,0:T(8,128)(2,1)} async-done(((bf16[256,768]{1,0:T(8,128)(2,1)}), bf16[2048,768]{1,0:T(8,128)(2,1)}) %all-gather.6.cloned.1.call-update) | async-done | bytes 3145744 | tf_op jit(solution)/shard_map/all_gather | solution.py:257
  44.3 1.6 copy-done.3
  47.2 6.9 %forward_products.1 = (bf16[4,8,64,768]{3,2,1,0:T(8,128)(2,1)S(1)}, bf16[4,8,64,768]{3,2,1,0:T(8,128)(2,1)}) custom-call(s32[64]{0:T(128)S(1)} %bitcast.50, s32[64]{0:T(128)S(1)} %bitcast.48, s32[1]{0:T(128)} %bitcast.43.count, bf16[64,128,128]{2,1,0:T(8,128)(2,1)S(1)} %bitcast.46, bf16[16,128,768]{2,1,0:T(8,128)(2,1)} %bitcast.65), custom_call_target="tpu_custom_call" | custom-call | flops 1610612736 | bytes 12000000 | tf_op jit(solution)/shard_map/forward_products/pallas_call | solution.py:90
  54.1 1.6 copy-done.2
  55.8 6.4 %all-to-all-start.2 = ((bf16[4,8,64,768]{3,2,1,0:T(8,128)(2,1)}), bf16[4,8,64,768]{3,2,1,0:T(8,128)(2,1)}, u32[]{:S(2)}, u32[]{:S(2)}) async-start(bf16[4,8,64,768]{3,2,1,0:T(8,128)(2,1)} %get-tuple-element.7), calls=%async_computation.3 | async-start | bytes 6291456 | tf_op jit(solution)/shard_map/all_to_all | solution.py:266
  62.9 37.1 %all-to-all-done.2.arrived = bf16[4,8,64,768]{3,2,1,0:T(8,128)(2,1)} async-done(((bf16[4,8,64,768]{3,2,1,0:T(8,128)(2,1)}), bf16[4,8,64,768]{3,2,1,0:T(8,128)(2,1)}, u32[]{:S(2)}, u32[]{:S(2)}) %all-to-all-start.2) | async-done | bytes 3145760 | tf_op jit(solution)/shard_map/all_to_all | solution.py:266
  100.0 6.2 %combine.3 = bf16[8,2,64,768]{3,2,1,0:T(8,128)(2,1)} custom-call(s32[4,8]{1,0:T(4,128)} %slice_reduce_fusion.2.asked, bf16[4,8,64,768]{3,2,1,0:T(8,128)(2,1)} %all-to-all-done.2.arrived), custom_call_target="tpu_custom_call" | custom-call | flops 12582912 | bytes 6000000 | tf_op jit(solution)/shard_map/combine/pallas_call | solution.py:178
  106.3 41.8 %all_to_all.35.arrived = bf16[4,8,64,768]{3,2,1,0:T(8,128)(2,1)} all-to-all(bf16[4,8,64,768]{3,2,1,0:T(8,128)(2,1)} %copy-done.2), channel_id=1, replica_groups=mesh['y'=4,'c'=2,'z'=8,'x'=4] {'x'}, dimensions={0} | all-to-all | bytes 6291456 | tf_op jit(solution)/shard_map/all_to_all | solution.py:266
  148.1 6.3 %combine.2 = bf16[8,2,64,768]{3,2,1,0:T(8,128)(2,1)} custom-call(s32[4,8]{1,0:T(4,128)} %slice_reduce_fusion.2.asked, bf16[4,8,64,768]{3,2,1,0:T(8,128)(2,1)} %all_to_all.35.arrived), custom_call_target="tpu_custom_call" | custom-call | flops 12582912 | bytes 6000000 | tf_op jit(solution)/shard_map/combine/pallas_call | solution.py:178
  154.4 1.0 copy-done.10
  155.5 1.4 fusion.12
  156.9 33.8 %reduce-scatter.5.cloned.1.call-done = bf16[128,768]{1,0:T(8,128)(2,1)} async-done(((bf16[1024,768]{1,0:T(8,128)(2,1)}), bf16[128,768]{1,0:T(8,128)(2,1)}) %reduce-scatter.5.cloned.1.call-update) | async-done | bytes 196624 | tf_op jit(solution)/shard_map/reduce_scatter | solution.py:268
  190.8 1.5 fusion.13
  192.3 1.8 convolution_convert_fusion
  194.1 1.3 convolution_convert_fusion.2
  195.6 1.3 convolution_convert_fusion.1
  197.0 32.9 %reduce-scatter.11.cloned.1.call-done = bf16[96,1024]{1,0:T(8,128)(2,1)} async-done(((bf16[768,1024]{1,0:T(8,128)(2,1)}), bf16[96,1024]{1,0:T(8,128)(2,1)}) %reduce-scatter.11.cloned.1.call-update) | async-done | bytes 196624 | tf_op jit(solution)/shard_map/reduce_scatter | solution.py:217
  229.9 1.1 reshape.162
  231.1 19.4 %all_to_all.36 = bf16[32,4,1024]{2,1,0:T(4,128)(2,1)S(1)} all-to-all(bf16[32,4,1024]{2,1,0:T(4,128)(2,1)S(1)} %fusion.8), channel_id=1, replica_groups=mesh['y'=4,'c'=2,'z'=8,'x'=4] {'z','x'}, dimensions={0} | all-to-all | bytes 524288 | tf_op jit(solution)/shard_map/all_to_all | solution.py:223
  251.5 3.9 all-to-all-start.6
  255.4 18.6 %all-gather.8.cloned.1.call-done = bf16[1024,768]{1,0:T(8,128)(2,1)} async-done(((bf16[128,768]{1,0:T(8,128)(2,1)}), bf16[1024,768]{1,0:T(8,128)(2,1)}) %all-gather.8.cloned.1.call-update) | async-done | bytes 1572880 | tf_op jit(solution)/shard_map/all_gather | solution.py:283
  273.9 5.8 %pick.2 = bf16[4,8,64,768]{3,2,1,0:T(8,128)(2,1)} custom-call(s32[4,8]{1,0:T(4,128)} %slice_reduce_fusion.2.asked, bf16[8,2,64,768]{3,2,1,0:T(8,128)(2,1)} %bitcast.58), custom_call_target="tpu_custom_call" | custom-call | flops 1572864 | bytes 6000000 | tf_op jit(solution)/shard_map/pick/pallas_call | solution.py:199
  279.8 4.7 %all-to-all-start.3 = ((bf16[4,8,64,768]{3,2,1,0:T(8,128)(2,1)}), bf16[4,8,64,768]{3,2,1,0:T(8,128)(2,1)}, u32[]{:S(2)}, u32[]{:S(2)}) async-start(bf16[4,8,64,768]{3,2,1,0:T(8,128)(2,1)} %pick.2), calls=%async_computation.5 | async-start | bytes 6291456 | tf_op jit(solution)/shard_map/all_to_all | solution.py:285
  285.6 29.1 %all-gather.10.cloned.1.call-done = bf16[1024,768]{1,0:T(8,128)(2,1)} async-done(((bf16[128,768]{1,0:T(8,128)(2,1)}), bf16[1024,768]{1,0:T(8,128)(2,1)}) %all-gather.10.cloned.1.call-update) | async-done | bytes 1572880 | tf_op jit(solution)/shard_map/all_gather | solution.py:283
  314.7 5.9 %pick.3 = bf16[4,8,64,768]{3,2,1,0:T(8,128)(2,1)} custom-call(s32[4,8]{1,0:T(4,128)} %slice_reduce_fusion.2.asked, bf16[8,2,64,768]{3,2,1,0:T(8,128)(2,1)} %bitcast.57), custom_call_target="tpu_custom_call" | custom-call | flops 1572864 | bytes 6000000 | tf_op jit(solution)/shard_map/pick/pallas_call | solution.py:199
  320.6 38.6 %all_to_all.37.rest_1_ = bf16[4,8,64,768]{3,2,1,0:T(8,128)(2,1)} all-to-all(bf16[4,8,64,768]{3,2,1,0:T(8,128)(2,1)} %pick.3), channel_id=1, replica_groups=mesh['y'=4,'c'=2,'z'=8,'x'=4] {'x'}, dimensions={0} | all-to-all | bytes 6291456 | tf_op jit(solution)/shard_map/all_to_all | solution.py:285
  359.2 5.6 %backward_products.1 = bf16[16,128,768]{2,1,0:T(8,128)(2,1)S(1)} custom-call(s32[64]{0:T(128)S(1)} %bitcast.51, s32[64]{0:T(128)S(1)} %bitcast.49, s32[1]{0:T(128)} %bitcast.44.count, bf16[64,128,128]{2,1,0:T(8,128)(2,1)S(1)} %bitcast.47, bf16[4,8,64,768]{3,2,1,0:T(8,128)(2,1)} %all-to-all-done.3.rest_0_, bf16[4,8,64,768]{3,2,1,0:T(8,128)(2,1)} %all_to_all.37.rest_1_), custom_call_target="tpu_custom_call" | custom-call | flops 1610612736 | bytes 12000000 | tf_op jit(solution)/shard_map/backward_products/pallas_call | solution.py:147
  364.8 1.6 copy-done.1
  366.5 0.8 pad_maximum_fusion
  367.3 3.6 slice.33
  371.9 38.3 %reduce-scatter.9.cloned.1.call-done = bf16[256,768]{1,0:T(8,128)(2,1)} async-done(((bf16[2048,768]{1,0:T(8,128)(2,1)}), bf16[256,768]{1,0:T(8,128)(2,1)}) %reduce-scatter.9.cloned.1.call-update) | async-done | bytes 393232 | tf_op jit(solution)/shard_map/reduce_scatter | solution.py:298
  (64 shorter events, 8.1 us)
Async XLA Ops:
  7.2 148.3 %copy-start = (bf16[768,1024]{1,0:T(8,128)(2,1)S(1)}, bf16[768,1024]{1,0:T(8,128)(2,1)}, u32[]{:S(2)}) copy-start(bf16[768,1024]{1,0:T(8,128)(2,1)} %param.13) | copy-start | bytes 4718596
  7.2 37.1 %all-gather.6.cloned.1.call-start = ((), (), s32[]{:S(2)}) async-start(), calls=%async_computation.11 | async-start | bytes 3538944 | tf_op jit(solution)/shard_map/all_gather | solution.py:257
  10.2 45.6 %all-to-all-start = ((s32[4,8,128]{2,1,0:T(8,128)}), s32[4,8,128]{2,1,0:T(8,128)S(1)}, u32[]{:S(2)}, u32[]{:S(2)}) async-start(s32[4,8,128]{2,1,0:T(8,128)} %broadcast_in_dim.18), calls=%async_computation | async-start | bytes 32768 | tf_op jit(solution)/shard_map/all_to_all | solution.py:253
  44.3 1.6 copy-start.3
  45.9 0.7 copy-start.5
  46.6 0.7 copy-start.7
  54.1 1.6 copy-start.2
  55.8 44.2 %all-to-all-start.2 = ((bf16[4,8,64,768]{3,2,1,0:T(8,128)(2,1)}), bf16[4,8,64,768]{3,2,1,0:T(8,128)(2,1)}, u32[]{:S(2)}, u32[]{:S(2)}) async-start(bf16[4,8,64,768]{3,2,1,0:T(8,128)(2,1)} %get-tuple-element.7), calls=%async_computation.3 | async-start | bytes 6291456 | tf_op jit(solution)/shard_map/all_to_all | solution.py:266
  62.2 93.3 %reduce-scatter.7.cloned.1.call-start = ((), (), s32[]{:S(2)}) async-start(), calls=%async_computation.13 | async-start | bytes 1769472 | tf_op jit(solution)/shard_map/reduce_scatter | solution.py:268
  106.2 84.5 %reduce-scatter.5.cloned.1.call-start = ((), (), s32[]{:S(2)}) async-start(), calls=%async_computation.12 | async-start | bytes 1769472 | tf_op jit(solution)/shard_map/reduce_scatter | solution.py:268
  154.3 1.0 copy-start.10
  154.3 1.1 copy-start.13
  154.4 75.5 %reduce-scatter.11.cloned.1.call-start = ((), (), s32[]{:S(2)}) async-start(), calls=%async_computation.17 | async-start | bytes 1769472 | tf_op jit(solution)/shard_map/reduce_scatter | solution.py:217
  190.8 1.5 copy-start.11
  190.8 1.5 copy-start.12
  194.1 79.9 %all-gather.8.cloned.1.call-start = ((), (), s32[]{:S(2)}) async-start(), calls=%async_computation.14 | async-start | bytes 1769472 | tf_op jit(solution)/shard_map/all_gather | solution.py:283
  195.5 119.2 %all-gather.10.cloned.1.call-start = ((), (), s32[]{:S(2)}) async-start(), calls=%async_computation.15 | async-start | bytes 1769472 | tf_op jit(solution)/shard_map/all_gather | solution.py:283
  251.5 28.3 %all-to-all-start.6 = ((bf16[32,4,1024]{2,1,0:T(4,128)(2,1)}), bf16[32,4,1024]{2,1,0:T(4,128)(2,1)S(1)}, u32[]{:S(2)}, u32[]{:S(2)}) async-start(bf16[32,4,1024]{2,1,0:T(4,128)(2,1)} %broadcast_in_dim.19), calls=%async_computation.10 | async-start | bytes 524288 | tf_op jit(solution)/shard_map/all_to_all | solution.py:225
  279.8 40.9 %all-to-all-start.3 = ((bf16[4,8,64,768]{3,2,1,0:T(8,128)(2,1)}), bf16[4,8,64,768]{3,2,1,0:T(8,128)(2,1)}, u32[]{:S(2)}, u32[]{:S(2)}) async-start(bf16[4,8,64,768]{3,2,1,0:T(8,128)(2,1)} %pick.2), calls=%async_computation.5 | async-start | bytes 6291456 | tf_op jit(solution)/shard_map/all_to_all | solution.py:285
  284.4 82.9 %all-gather.12.cloned.1.call-start = ((), (), s32[]{:S(2)}) async-start(), calls=%async_computation.18 | async-start | bytes 2064384 | tf_op jit(solution)/shard_map/all_gather | solution.py:231
  285.5 124.7 %reduce-scatter.9.cloned.1.call-start = ((), (), s32[]{:S(2)}) async-start(), calls=%async_computation.16 | async-start | bytes 3538944 | tf_op jit(solution)/shard_map/reduce_scatter | solution.py:298
  320.6 38.6 %copy-start.6 = (s32[1,1,64]{2,1,0:T(1,128)S(1)}, s32[1,1,64]{2,1,0:T(1,128)}, u32[]{:S(2)}) copy-start(s32[1,1,64]{2,1,0:T(1,128)} %param.11) | copy-start | bytes 772
  320.6 38.6 %copy-start.8 = (s32[1,1,64]{2,1,0:T(1,128)S(1)}, s32[1,1,64]{2,1,0:T(1,128)}, u32[]{:S(2)}) copy-start(s32[1,1,64]{2,1,0:T(1,128)} %param.10) | copy-start | bytes 772
  320.6 38.6 %copy-start.4 = (bf16[1,1,64,128,128]{4,3,2,1,0:T(8,128)(2,1)S(1)}, bf16[1,1,64,128,128]{4,3,2,1,0:T(8,128)(2,1)}, u32[]{:S(2)}) copy-start(bf16[1,1,64,128,128]{4,3,2,1,0:T(8,128)(2,1)} %param.9) | copy-start | bytes 6291460
  364.8 1.6 copy-start.1
  367.3 3.6 copy-start.9
Sparse Core Ops, SparseCore 0:
  9.8 34.4 all-gather.5
  106.4 37.2 reduce-scatter.6
  154.5 36.2 reduce-scatter.4
  194.2 35.6 reduce-scatter.10
  232.1 41.7 all-gather.7
  275.6 39.0 all-gather.9
  316.5 30.2 all-gather.11
  366.6 43.6 reduce-scatter.8
